TPU v7x, 512 devices: a whole 4x8x8 slice. The times are simulated.
512 devices in a mesh: row: 16 (over y_lo, x, core), col: 32 (over y_hi, z).
Axes of the slice: x: 4, y: 8 (y_hi: 4, y_lo: 2; y = y_hi * 2 + y_lo), z: 8, core: 2. Of those that a mesh axis runs over, the one named last changes fastest.
Arguments:
- object_field: float32 [2, 4096, 8192], P(None, 'row', 'col'), may hold values from -6 to 6
- probe: float32 [2, 128, 128], replicated, may hold values from -6 to 6
- amplitude: bfloat16 [16, 32, 16, 128, 128], P('row', 'col'), may hold values from 0 to 2
- corners: int32 [2, 16, 32, 16], P(None, 'row', 'col'), may hold values from 0 to 255, as said below
- live_count: int32 [16, 32], P('row', 'col'), may hold values from 4 to 16, as said below
Outputs:
- refined_object: float32 [2, 4096, 8192], P(None, 'row', 'col')
- new_probe: float32 [2, 128, 128], replicated
Inputs may be any that keep to these rules, and one draw needn't show every extreme that they name: In the last tile row of the mesh corners[0] is at most 128, and in the last tile column corners[1] is at most 128, so every window lies inside the object. Outside the last tile row, corners[0] of slot 0 is at least 192; outside the last tile column, corners[1] of slot 0 is at least 192. Unused slots carry valid corners. Slots from live_count on are unused. Some tile uses all 16 slots in every draw.
All inputs are finite; a program needn't handle non-finite values.
Results may differ from a plain program's by a relative error of at most 0.0039.
The roundings to bfloat16 on the way count: a program that leaves them out, or rounds other values in their place, can miss the bound.
Values may be sent and summed in bfloat16 or wider, within the bound.
No kernel may reach another device: no remote copies, remote signals or barrier semaphores. Data moves between devices by JAX's collectives and lax.ppermute only.
A program may use at most 64 MiB of HBM per device.

v0:
```python
import math
import jax
import jax.numpy as jnp
from jax import lax
from jax.sharding import PartitionSpec as P

BLOCK = 4


def from_behind(value, axis, steps):
    count = lax.axis_size(axis)
    first, last = (max(0, -steps), min(count, count - steps))
    return lax.ppermute(value, axis, [(source, source + steps) for source in range(first, last)])


def dft_tables(window):
    indices = jnp.arange(window, dtype=jnp.int32)
    phase_index = indices[:, None] * indices[None, :] % window
    angles = phase_index.astype(jnp.float32) * (2.0 * math.pi / window)
    norming = 1.0 / math.sqrt(window)
    cosines = jnp.cos(angles) * norming
    sines = jnp.sin(angles) * norming
    forward_fourier = jnp.stack([jnp.stack([cosines, -sines]), jnp.stack([sines, cosines])])
    inverse_fourier = jnp.stack([jnp.stack([cosines, sines]), jnp.stack([-sines, cosines])])
    return (forward_fourier.astype(jnp.bfloat16), inverse_fourier.astype(jnp.bfloat16))


def times(left_value, right_value):
    real_part = (
        left_value[..., 0, :, :] * right_value[..., 0, :, :]
        - left_value[..., 1, :, :] * right_value[..., 1, :, :]
    )
    imag_part = (
        left_value[..., 0, :, :] * right_value[..., 1, :, :]
        + left_value[..., 1, :, :] * right_value[..., 0, :, :]
    )
    return jnp.stack([real_part, imag_part], -3)


def times_conj(left_value, right_value):
    real_part = (
        left_value[..., 0, :, :] * right_value[..., 0, :, :]
        + left_value[..., 1, :, :] * right_value[..., 1, :, :]
    )
    imag_part = (
        left_value[..., 0, :, :] * right_value[..., 1, :, :]
        - left_value[..., 1, :, :] * right_value[..., 0, :, :]
    )
    return jnp.stack([real_part, imag_part], -3)


def refine_object(exit_waves, measured_intensity, forward_fourier, inverse_fourier):
    half_done = jnp.einsum(
        "bcrk,cdkm->bdrm", exit_waves, forward_fourier, preferred_element_type=jnp.float32
    ).astype(jnp.bfloat16)
    spectrum = jnp.einsum(
        "cdrs,bcsm->bdrm", forward_fourier, half_done, preferred_element_type=jnp.float32
    )
    modulus = jnp.sqrt(spectrum[:, 0] * spectrum[:, 0] + spectrum[:, 1] * spectrum[:, 1])
    rescale = measured_intensity.astype(jnp.float32) / jnp.maximum(modulus, 0.5)
    projected = (spectrum * rescale[:, None]).astype(jnp.bfloat16)
    half_back = jnp.einsum(
        "bcrk,cdkm->bdrm", projected, inverse_fourier, preferred_element_type=jnp.float32
    ).astype(jnp.bfloat16)
    returned = jnp.einsum(
        "cdrs,bcsm->bdrm", inverse_fourier, half_back, preferred_element_type=jnp.float32
    )
    return returned - exit_waves.astype(jnp.float32)


def refine_all(exit_waves, measured_intensity, update_marks, forward_fourier, inverse_fourier):
    group_size = BLOCK
    turns = exit_waves.shape[0] // group_size
    collected = jnp.zeros(exit_waves.shape, jnp.float32)

    def advance(position, collected):
        offset = position * group_size
        exit_wave_portion = lax.dynamic_slice_in_dim(exit_waves, offset, group_size, 0)
        measured_part = lax.dynamic_slice_in_dim(measured_intensity, offset, group_size, 0)
        any_used = jnp.any(lax.dynamic_slice_in_dim(update_marks, offset, group_size, 0))
        object_delta = lax.cond(
            any_used,
            lambda exit_wave_current, measurement_current: refine_object(
                exit_wave_current, measurement_current, forward_fourier, inverse_fourier
            ),
            lambda exit_wave_current, measurement_current: jnp.zeros(
                exit_wave_current.shape, jnp.float32
            ),
            exit_wave_portion,
            measured_part,
        )
        return lax.dynamic_update_slice_in_dim(collected, object_delta, offset, 0)

    return lax.fori_loop(0, turns, advance, collected)


def extend(current, window):
    right_rim = from_behind(current[:, :, :window], "col", -1)
    lower_rim = from_behind(current[:, :window, :], "row", -1)
    corner_rim = from_behind(
        current[:, :window, :window], ("row", "col"), -(lax.axis_size("col") + 1)
    )
    widened = jnp.concatenate([current, right_rim], 2)
    lower_wide = jnp.concatenate([lower_rim, corner_rim], 2)
    return jnp.concatenate([widened, lower_wide], 1)


def fold(deposit, window):
    tile_size = deposit.shape[1] - window
    spilled = from_behind(deposit[:, tile_size:, :tile_size], "row", 1)
    right_part = from_behind(deposit[:, :tile_size, tile_size:], "col", 1)
    corner_part = from_behind(
        deposit[:, tile_size:, tile_size:], ("row", "col"), lax.axis_size("col") + 1
    )
    result = deposit[:, :tile_size, :tile_size]
    result = result.at[:, :window, :].add(spilled)
    result = result.at[:, :, :window].add(right_part)
    return result.at[:, :window, :window].add(corner_part)


def sweep(
    current,
    probe,
    work_measured,
    used,
    work_used,
    corner_list,
    forward_fourier,
    inverse_fourier,
    with_light,
):
    window = probe.shape[1]
    tile_size = current.shape[1]
    slots = used.shape[0]
    extended = extend(current, window)
    zero_index = jnp.zeros((), jnp.int32)

    def cut_patch(spot):
        return lax.dynamic_slice(extended, (zero_index, spot[0], spot[1]), (2, window, window))

    patches = jax.vmap(cut_patch)(corner_list)
    exit_waves = times(probe[None], patches).astype(jnp.bfloat16)
    object_delta = refine_all(
        exit_waves, work_measured, work_used, forward_fourier, inverse_fourier
    )
    weights = used.astype(jnp.float32)
    object_delta = object_delta * weights[:, None, None, None]
    pushed = times_conj(probe[None], object_delta)
    if with_light:
        power = probe[0] * probe[0] + probe[1] * probe[1]
        lighting = power[None] * weights[:, None, None]
        pushed = jnp.concatenate([pushed, lighting[:, None]], 1)
    channels = pushed.shape[1]
    deposit = jnp.zeros((channels, tile_size + window, tile_size + window), jnp.float32)

    def place(position, deposit):
        spot = corner_list[position]
        anchor = (zero_index, spot[0], spot[1])
        present = lax.dynamic_slice(deposit, anchor, (channels, window, window))
        return lax.dynamic_update_slice(deposit, present + pushed[position], anchor)

    deposit = lax.fori_loop(0, slots, place, deposit)
    gathered = fold(deposit, window)
    gradient = None
    if not with_light:
        gradient = jnp.sum(times_conj(patches, object_delta), 0)
    return (gathered, gradient)


def on_device(object_field, probe, amplitude, corners, live_count):
    slots = amplitude.shape[2]
    window = probe.shape[1]
    measured_intensity = amplitude.reshape(slots, window, window)
    corner_list = jnp.transpose(corners.reshape(2, slots))
    used = jnp.arange(slots, dtype=jnp.int32) < live_count.reshape(())
    forward_fourier, inverse_fourier = dft_tables(window)
    first_pass, unused_grad = sweep(
        object_field,
        probe,
        measured_intensity,
        used,
        used,
        corner_list,
        forward_fourier,
        inverse_fourier,
        True,
    )
    denominator = first_pass[2] + 4.0
    updated = object_field + first_pass[:2] / denominator
    second_pass, gradient = sweep(
        updated,
        probe,
        measured_intensity,
        used,
        used,
        corner_list,
        forward_fourier,
        inverse_fourier,
        False,
    )
    refined_object = updated + second_pass / denominator
    summed = lax.psum(gradient, ("row", "col"))
    spread = jnp.sqrt(jnp.mean(summed[0] * summed[0] + summed[1] * summed[1]) + 1e-06)
    new_probe = probe + summed / spread
    return (refined_object, new_probe)


def solution(mesh):
    in_specs = (
        P(None, "row", "col"),
        P(),
        P("row", "col", None, None, None),
        P(None, "row", "col", None),
        P("row", "col"),
    )
    out_specs = (P(None, "row", "col"), P())
    return jax.shard_map(
        on_device, mesh=mesh, in_specs=in_specs, out_specs=out_specs, check_vma=False
    )
```

profile of v0, /device:TPU:1, one launch (start us, length us, event | category | flops | bytes accessed | tf_op | source)
XLA Modules:
  0.0 658.6 jit_solution(6017470516622135121)
XLA Ops:
  10.5 8.9 %collective-permute-start.1 = (f32[2,128,256]{2,1,0:T(8,128)S(1)}, f32[2,128,256]{2,1,0:T(8,128)S(1)}, u32[]{:S(2)}, u32[]{:S(2)}) collective-permute-start(f32[2,128,256]{2,1,0:T(8,128)S(1)} %slice.346), channel_id=1, source_target_pairs={{32,0},{64,32},{96,64},{128,96},{160,128},{192,160},{224,192},{256... | collective-permute-start | bytes 786440 | tf_op jit(solution)/shard_map/ppermute | solution.py:13
  28.9 49.5 %while.64 = (s32[]{:T(128)}, f32[2,384,384]{2,1,0:T(8,128)}, s32[16,3]{0,1:T(4,128)S(1)}, f32[16,2,128,128]{3,2,1,0:T(8,128)S(1)}, s32[]{:T(128)}) while((s32[]{:T(128)}, f32[2,384,384]{2,1,0:T(8,128)}, s32[16,3]{0,1:T(4,128)S(1)}, f32[16,2,128,128]{3,2,1,0:T(8,128)S(1)}, s32[]{:T(128)}) %tuple.206), condition=%wide.while_cond.6, body=%wide.while_body.6.sunk | while | flops 2 | bytes 262261 | solution.py:139
  81.0 12.3 %while.60 = (s32[]{:T(128)}, f32[16,2,128,128]{3,2,1,0:T(8,128)}, pred[16]{0:T(512)(128)(4,1)S(1)}, bf16[16,2,128,128]{2,3,1,0:T(8,128)(2,1)S(1)}, bf16[2,2,128,...) while((s32[]{:T(128)}, f32[16,2,128,128]{3,2,1,0:T(8,128)}, ...), condition=%wide.region_4.5_spmd, body=%wide.region_0.4_spmd.sunk | while | flops 269615104 | bytes 5898981 | solution.py:94
  98.6 137.3 %while.61 = (s32[]{:T(128)}, f32[3,384,384]{2,1,0:T(8,128)S(1)}, s32[16,2]{0,1:T(2,128)S(1)}, f32[16,3,128,128]{3,2,1,0:T(8,128)}, s32[]{:T(128)}, /*index=5*/s32[]{:T(128)}, s32[]{:T(128)}) while((s32[]{:T(128)}, f32[3,384,384]{2,1,0:T(8,128)S(1)}, s32[16,2]{0,1:T(2,128)S(1)}, f32[16,3,128,128]{3,2,1,0:T(8,128)}, s32[]{:T(128)}, ...), condition=%wide.region_6.7_spmd, body=%wide.region_5.6_spmd.sunk | while | flops 49160 | bytes 983237 | solution.py:162
  104.3 2.7 dynamic_update_slice.35
  112.7 3.1 dynamic_update_slice.35
  129.0 3.1 dynamic_update_slice.35
  137.7 3.1 dynamic_update_slice.35
  146.4 3.1 dynamic_update_slice.35
  155.2 2.9 dynamic_update_slice.35
  163.7 2.8 dynamic_update_slice.35
  172.2 3.0 dynamic_update_slice.35
  180.9 2.9 dynamic_update_slice.35
  189.4 3.1 dynamic_update_slice.35
  198.2 2.7 dynamic_update_slice.35
  206.6 3.1 dynamic_update_slice.35
  215.3 3.0 dynamic_update_slice.35
  224.1 3.1 dynamic_update_slice.35
  232.8 3.1 dynamic_update_slice.35
  235.9 11.9 %collective-permute-start.3 = (f32[3,128,256]{2,1,0:T(8,128)S(1)}, f32[3,128,256]{2,1,0:T(8,128)S(1)}, u32[]{:S(2)}, u32[]{:S(2)}) collective-permute-start(f32[3,128,256]{2,1,0:T(8,128)S(1)} %slice.359), channel_id=1, source_target_pairs={{0,32},{32,64},{64,96},{96,128},{128,160},{160,192},{192,224},{224... | collective-permute-start | bytes 1179656 | tf_op jit(solution)/shard_map/ppermute | solution.py:13
  252.6 5.2 collective-permute-done.4
  264.6 16.0 %collective-permute-done.8 = f32[2,128,128]{2,1,0:T(8,128)S(1)} collective-permute-done((f32[2,128,128]{2,1,0:T(8,128)S(1)}, f32[2,128,128]{2,1,0:T(8,128)S(1)}, u32[]{:S(2)}, u32[]{:S(2)}) %collective-permute-start.8) | collective-permute-done | bytes 131104 | tf_op jit(solution)/shard_map/ppermute | solution.py:13
  282.0 49.1 %while.65 = (s32[]{:T(128)}, f32[2,384,384]{2,1,0:T(8,128)}, s32[16,3]{0,1:T(4,128)S(1)}, f32[16,2,128,128]{3,2,1,0:T(8,128)S(1)}, s32[]{:T(128)}) while((s32[]{:T(128)}, f32[2,384,384]{2,1,0:T(8,128)}, s32[16,3]{0,1:T(4,128)S(1)}, f32[16,2,128,128]{3,2,1,0:T(8,128)S(1)}, s32[]{:T(128)}) %tuple.235), condition=%wide.while_cond.7, body=%wide.while_body.7.sunk | while | flops 2 | bytes 262261 | solution.py:139
  336.6 13.6 %while.62 = (s32[]{:T(128)}, f32[16,2,128,128]{3,2,1,0:T(8,128)}, pred[16]{0:T(512)(128)(4,1)S(1)}, bf16[16,2,128,128]{2,3,1,0:T(8,128)(2,1)S(1)}, bf16[2,2,128,...) while((s32[]{:T(128)}, f32[16,2,128,128]{3,2,1,0:T(8,128)}, ...), condition=%wide.region_11.12_spmd, body=%wide.region_7.11_spmd.sunk | while | flops 269615104 | bytes 5898981 | solution.py:94
  355.6 125.7 %while.63 = (s32[]{:T(128)}, f32[2,384,384]{2,1,0:T(8,128)S(1)}, s32[16,2]{0,1:T(2,128)S(1)}, f32[16,2,128,128]{3,2,1,0:T(8,128)}, s32[]{:T(128)}, /*index=5*/s32[]{:T(128)}, s32[]{:T(128)}) while((s32[]{:T(128)}, f32[2,384,384]{2,1,0:T(8,128)S(1)}, s32[16,2]{0,1:T(2,128)S(1)}, f32[16,2,128,128]{3,2,1,0:T(8,128)}, s32[]{:T(128)}, ...), condition=%wide.region_13.14_spmd, body=%wide.region_12.13_spmd.sunk | while | flops 32776 | bytes 655557 | solution.py:162
  368.7 2.5 dynamic_update_slice.37
  383.9 2.5 dynamic_update_slice.37
  391.9 2.5 dynamic_update_slice.37
  399.9 2.5 dynamic_update_slice.37
  439.2 2.5 dynamic_update_slice.37
  482.2 7.6 %collective-permute-start.9 = (f32[2,128,256]{2,1,0:T(8,128)}, f32[2,128,256]{2,1,0:T(8,128)S(1)}, u32[]{:S(2)}, u32[]{:S(2)}) collective-permute-start(f32[2,128,256]{2,1,0:T(8,128)} %slice.375), channel_id=1, source_target_pairs={{0,32},{32,64},{64,96},{96,128},{128,160},{160,192},{192,224},{224... | collective-permute-start | bytes 786440 | tf_op jit(solution)/shard_map/ppermute | solution.py:13
  493.0 153.0 %all-reduce.2.cloned.1.call-done = f32[2,128,128]{2,1,0:T(8,128)} async-done(((f32[2,128,128]{2,1,0:T(8,128)}), f32[2,128,128]{2,1,0:T(8,128)}) %all-reduce.2.cloned.1.call-update) | async-done | bytes 131088 | tf_op jit(solution)/shard_map/psum | solution.py:202
  (353 shorter events, 258.1 us)
Async XLA Ops:
  7.2 19.4 %copy-start.8 = (bf16[1,1,16,128,128]{4,3,2,1,0:T(8,128)(2,1)S(1)}, bf16[1,1,16,128,128]{4,3,2,1,0:T(8,128)(2,1)}, u32[]{:S(2)}) copy-start(bf16[1,1,16,128,128]{4,3,2,1,0:T(8,128)(2,1)} %param.31) | copy-start | bytes 1572868
  7.2 638.8 %all-reduce.2.cloned.1.call-start = ((), (), s32[]{:S(2)}) async-start(), calls=%async_computation | async-start | bytes 262144 | tf_op jit(solution)/shard_map/psum | solution.py:202
  8.2 19.3 %collective-permute-start = (f32[2,256,128]{2,1,0:T(8,128)S(1)}, f32[2,256,128]{2,1,0:T(8,128)S(1)}, u32[]{:S(2)}, u32[]{:S(2)}) collective-permute-start(f32[2,256,128]{2,1,0:T(8,128)S(1)} %slice.345), channel_id=1, source_target_pairs={{1,0},{2,1},{3,2},{4,3},{5,4},{6,5},{7,6},{8,7},{9,8},{10,9},{11,1... | collective-permute-start | bytes 786440 | tf_op jit(solution)/shard_map/ppermute | solution.py:13
  10.5 17.0 %copy-start.4 = (f32[2,256,256]{2,1,0:T(8,128)S(1)}, f32[2,256,256]{2,1,0:T(8,128)}, u32[]{:S(2)}) copy-start(f32[2,256,256]{2,1,0:T(8,128)} %param.29) | copy-start | bytes 1572868
  10.5 17.0 %collective-permute-start.1 = (f32[2,128,256]{2,1,0:T(8,128)S(1)}, f32[2,128,256]{2,1,0:T(8,128)S(1)}, u32[]{:S(2)}, u32[]{:S(2)}) collective-permute-start(f32[2,128,256]{2,1,0:T(8,128)S(1)} %slice.346), channel_id=1, source_target_pairs={{32,0},{64,32},{96,64},{128,96},{160,128},{192,160},{224,192},{256... | collective-permute-start | bytes 786440 | tf_op jit(solution)/shard_map/ppermute | solution.py:13
  20.3 7.2 %collective-permute-start.2 = (f32[2,128,128]{2,1,0:T(8,128)S(1)}, f32[2,128,128]{2,1,0:T(8,128)S(1)}, u32[]{:S(2)}, u32[]{:S(2)}) collective-permute-start(f32[2,128,128]{2,1,0:T(8,128)S(1)} %slice.347), channel_id=1, source_target_pairs={{33,0},{34,1},{35,2},{36,3},{37,4},{38,5},{39,6},{40,7},{41,8},{42... | collective-permute-start | bytes 393224 | tf_op jit(solution)/shard_map/ppermute | solution.py:13
  93.3 2.1 copy-start.3
  95.4 1.2 copy-start.6
  96.6 2.0 copy-start.9
  235.9 16.6 %collective-permute-start.3 = (f32[3,128,256]{2,1,0:T(8,128)S(1)}, f32[3,128,256]{2,1,0:T(8,128)S(1)}, u32[]{:S(2)}, u32[]{:S(2)}) collective-permute-start(f32[3,128,256]{2,1,0:T(8,128)S(1)} %slice.359), channel_id=1, source_target_pairs={{0,32},{32,64},{64,96},{96,128},{128,160},{160,192},{192,224},{224... | collective-permute-start | bytes 1179656 | tf_op jit(solution)/shard_map/ppermute | solution.py:13
  247.9 9.9 %collective-permute-start.4 = (f32[3,256,128]{2,1,0:T(8,128)S(1)}, f32[3,256,128]{2,1,0:T(8,128)S(1)}, u32[]{:S(2)}, u32[]{:S(2)}) collective-permute-start(f32[3,256,128]{2,1,0:T(8,128)S(1)} %slice.361), channel_id=1, source_target_pairs={{0,1},{1,2},{2,3},{3,4},{4,5},{5,6},{6,7},{7,8},{8,9},{9,10},{10,1... | collective-permute-start | bytes 1179656 | tf_op jit(solution)/shard_map/ppermute | solution.py:13
  249.3 10.7 %copy-start.5 = (f32[2,256,256]{2,1,0:T(8,128)S(1)}, f32[2,256,256]{2,1,0:T(8,128)}, u32[]{:S(2)}) copy-start(f32[2,256,256]{2,1,0:T(8,128)} %param.29) | copy-start | bytes 1572868
  249.3 10.6 %collective-permute-start.5 = (f32[3,128,128]{2,1,0:T(8,128)S(1)}, f32[3,128,128]{2,1,0:T(8,128)S(1)}, u32[]{:S(2)}, u32[]{:S(2)}) collective-permute-start(f32[3,128,128]{2,1,0:T(8,128)S(1)} %slice.363), channel_id=1, source_target_pairs={{0,33},{1,34},{2,35},{3,36},{4,37},{5,38},{6,39},{7,40},{8,41},{9,... | collective-permute-start | bytes 589832 | tf_op jit(solution)/shard_map/ppermute | solution.py:13
  260.1 20.6 %collective-permute-start.6 = (f32[2,256,128]{2,1,0:T(8,128)S(1)}, f32[2,256,128]{2,1,0:T(8,128)S(1)}, u32[]{:S(2)}, u32[]{:S(2)}) collective-permute-start(f32[2,256,128]{2,1,0:T(8,128)S(1)} %slice.424), channel_id=1, source_target_pairs={{1,0},{2,1},{3,2},{4,3},{5,4},{6,5},{7,6},{8,7},{9,8},{10,9},{11,1... | collective-permute-start | bytes 786440 | tf_op jit(solution)/shard_map/ppermute | solution.py:13
  261.4 19.3 %collective-permute-start.7 = (f32[2,128,256]{2,1,0:T(8,128)S(1)}, f32[2,128,256]{2,1,0:T(8,128)S(1)}, u32[]{:S(2)}, u32[]{:S(2)}) collective-permute-start(f32[2,128,256]{2,1,0:T(8,128)S(1)} %slice.425), channel_id=1, source_target_pairs={{32,0},{64,32},{96,64},{128,96},{160,128},{192,160},{224,192},{256... | collective-permute-start | bytes 786440 | tf_op jit(solution)/shard_map/ppermute | solution.py:13
  263.3 17.3 %collective-permute-start.8 = (f32[2,128,128]{2,1,0:T(8,128)S(1)}, f32[2,128,128]{2,1,0:T(8,128)S(1)}, u32[]{:S(2)}, u32[]{:S(2)}) collective-permute-start(f32[2,128,128]{2,1,0:T(8,128)S(1)} %slice.426), channel_id=1, source_target_pairs={{33,0},{34,1},{35,2},{36,3},{37,4},{38,5},{39,6},{40,7},{41,8},{42... | collective-permute-start | bytes 393224 | tf_op jit(solution)/shard_map/ppermute | solution.py:13
  331.1 1.6 copy-start
  335.0 1.6 copy-start.2
  350.1 2.2 copy-start.1
  481.3 166.8 %copy-start.7 = (f32[2,128,128]{2,1,0:T(8,128)S(1)}, f32[2,128,128]{2,1,0:T(8,128)}, u32[]{:S(2)}) copy-start(f32[2,128,128]{2,1,0:T(8,128)} %param.30) | copy-start | bytes 393220
  482.2 167.6 %collective-permute-start.9 = (f32[2,128,256]{2,1,0:T(8,128)}, f32[2,128,256]{2,1,0:T(8,128)S(1)}, u32[]{:S(2)}, u32[]{:S(2)}) collective-permute-start(f32[2,128,256]{2,1,0:T(8,128)} %slice.375), channel_id=1, source_target_pairs={{0,32},{32,64},{64,96},{96,128},{128,160},{160,192},{192,224},{224... | collective-permute-start | bytes 786440 | tf_op jit(solution)/shard_map/ppermute | solution.py:13
  489.7 160.1 %collective-permute-start.10 = (f32[2,256,128]{2,1,0:T(8,128)S(1)}, f32[2,256,128]{2,1,0:T(8,128)}, u32[]{:S(2)}, u32[]{:S(2)}) collective-permute-start(f32[2,256,128]{2,1,0:T(8,128)S(1)} %slice.377), channel_id=1, source_target_pairs={{0,1},{1,2},{2,3},{3,4},{4,5},{5,6},{6,7},{7,8},{8,9},{9,10},{10,1... | collective-permute-start | bytes 786440 | tf_op jit(solution)/shard_map/ppermute | solution.py:13
  491.7 159.1 %collective-permute-start.11 = (f32[2,128,128]{2,1,0:T(8,128)S(1)}, f32[2,128,128]{2,1,0:T(8,128)S(1)}, u32[]{:S(2)}, u32[]{:S(2)}) collective-permute-start(f32[2,128,128]{2,1,0:T(8,128)S(1)} %slice.379), channel_id=1, source_target_pairs={{0,33},{1,34},{2,35},{3,36},{4,37},{5,38},{6,39},{7,40},{8,41},{9,... | collective-permute-start | bytes 393224 | tf_op jit(solution)/shard_map/ppermute | solution.py:13
Sparse Core Ops, SparseCore 0:
  354.1 291.8 all-reduce.1
where the time goes:
time: 664 us; the launch traced here: 659 us
  local copies, waits for them, and re-layouts  224 us (34%)
  waiting for transfers between devices  179 us (27%)
  loops' own time  132 us (20%)
  other arithmetic  63.8 us (10%)
  starting transfers between devices  41.5 us (6%)
  between operations  15.9 us (2%)
    psum x1, waiting for transfers between devices, on_device(): summed = lax.psum(gradient, ('row', 'col'))  153 us
    another operation x2, loops' own time, sweep(): deposit = lax.fori_loop(0, slots, place, deposit)  125 us
    gather x96, local copies, waits for them, and re-layouts  98 us
    dynamic_update_slice x32, local copies, waits for them, and re-layouts, place(): return lax.dynamic_update_slice(deposit, present + pushed[position], anchor)  83.9 us
    ppermute x12, starting transfers between devices, from_behind(): lax.ppermute(value, axis, [(source, source + steps) for source in range(f...  41.4 us
    add x32, other arithmetic, place(): return lax.dynamic_update_slice(deposit, present + pushed[position], anchor)  33.2 us
    ppermute x12, waiting for transfers between devices, from_behind(): lax.ppermute(value, axis, [(source, source + steps) for source in range(f...  25.5 us
    slice x32, local copies, waits for them, and re-layouts, place(): anchor = (zero_index, spot[0], spot[1])  18.3 us
  transfers between devices with their start and end apart: 13, of which 6 were waited for; matrix products, arithmetic and copies ran while one was open for 12% of the time, Pallas kernels for 0%

commit v1 on v0

--- a/solution.py
+++ b/solution.py
@@ -199,7 +199,8 @@
         False,
     )
     refined_object = updated + second_pass / denominator
-    summed = lax.psum(gradient, ("row", "col"))
+    one_axis = lax.psum(gradient, "col")
+    summed = lax.psum(one_axis, "row")
     spread = jnp.sqrt(jnp.mean(summed[0] * summed[0] + summed[1] * summed[1]) + 1e-06)
     new_probe = probe + summed / spread
     return (refined_object, new_probe)

time: 664 us -> 835 us (1.26)
  the two profiles are of different devices: /device:TPU:1 before, /device:TPU:43 now
where the time goes in v1:
time: 835 us; the launch traced here: 830 us
  waiting for transfers between devices  339 us (41%)
  local copies, waits for them, and re-layouts  224 us (27%)
  loops' own time  132 us (16%)
  other arithmetic  63.8 us (8%)
  starting transfers between devices  52 us (6%)
  between operations  15.9 us (2%)
    psum x1, waiting for transfers between devices, on_device(): one_axis = lax.psum(gradient, 'col')  280 us
    another operation x2, loops' own time, sweep(): deposit = lax.fori_loop(0, slots, place, deposit)  126 us
    gather x96, local copies, waits for them, and re-layouts  98 us
    dynamic_update_slice x32, local copies, waits for them, and re-layouts, place(): return lax.dynamic_update_slice(deposit, present + pushed[position], anchor)  84.1 us
    ppermute x12, waiting for transfers between devices, from_behind(): lax.ppermute(value, axis, [(source, source + steps) for source in range(f...  59.2 us
    ppermute x12, starting transfers between devices, from_behind(): lax.ppermute(value, axis, [(source, source + steps) for source in range(f...  51.9 us
    add x32, other arithmetic, place(): return lax.dynamic_update_slice(deposit, present + pushed[position], anchor)  33.2 us
    slice x32, local copies, waits for them, and re-layouts, place(): anchor = (zero_index, spot[0], spot[1])  17.9 us
  transfers between devices with their start and end apart: 14, of which 8 were waited for; matrix products, arithmetic and copies ran while one was open for 9% of the time, Pallas kernels for 0%

profile of v1, /device:TPU:43, one launch (start us, length us, event | category | flops | bytes accessed | tf_op | source)
XLA Modules:
  0.0 830.3 jit_solution(5145954199344798090)
XLA Ops:
  8.2 11.3 %collective-permute-start = (f32[2,256,128]{2,1,0:T(8,128)S(1)}, f32[2,256,128]{2,1,0:T(8,128)S(1)}, u32[]{:S(2)}, u32[]{:S(2)}) collective-permute-start(f32[2,256,128]{2,1,0:T(8,128)S(1)} %slice.345), channel_id=1, source_target_pairs={{1,0},{2,1},{3,2},{4,3},{5,4},{6,5},{7,6},{8,7},{9,8},{10,9},{11,1... | collective-permute-start | bytes 786440 | tf_op jit(solution)/shard_map/ppermute | solution.py:13
  20.6 3.0 collective-permute-start.1
  35.1 49.5 %while.64 = (s32[]{:T(128)}, f32[2,384,384]{2,1,0:T(8,128)}, s32[16,3]{0,1:T(4,128)S(1)}, f32[16,2,128,128]{3,2,1,0:T(8,128)S(1)}, s32[]{:T(128)}) while((s32[]{:T(128)}, f32[2,384,384]{2,1,0:T(8,128)}, s32[16,3]{0,1:T(4,128)S(1)}, f32[16,2,128,128]{3,2,1,0:T(8,128)S(1)}, s32[]{:T(128)}) %tuple.206), condition=%wide.while_cond.6, body=%wide.while_body.6.sunk | while | flops 2 | bytes 262261 | solution.py:139
  87.3 12.3 %while.60 = (s32[]{:T(128)}, f32[16,2,128,128]{3,2,1,0:T(8,128)}, pred[16]{0:T(512)(128)(4,1)S(1)}, bf16[16,2,128,128]{2,3,1,0:T(8,128)(2,1)S(1)}, bf16[2,2,128,...) while((s32[]{:T(128)}, f32[16,2,128,128]{3,2,1,0:T(8,128)}, ...), condition=%wide.region_4.5_spmd, body=%wide.region_0.4_spmd.sunk | while | flops 269615104 | bytes 5898981 | solution.py:94
  104.8 137.4 %while.61 = (s32[]{:T(128)}, f32[3,384,384]{2,1,0:T(8,128)S(1)}, s32[16,2]{0,1:T(2,128)S(1)}, f32[16,3,128,128]{3,2,1,0:T(8,128)}, s32[]{:T(128)}, /*index=5*/s32[]{:T(128)}, s32[]{:T(128)}) while((s32[]{:T(128)}, f32[3,384,384]{2,1,0:T(8,128)S(1)}, s32[16,2]{0,1:T(2,128)S(1)}, f32[16,3,128,128]{3,2,1,0:T(8,128)}, s32[]{:T(128)}, ...), condition=%wide.region_6.7_spmd, body=%wide.region_5.6_spmd.sunk | while | flops 49160 | bytes 983237 | solution.py:162
  110.5 2.7 dynamic_update_slice.35
  118.9 3.0 dynamic_update_slice.35
  134.9 3.1 dynamic_update_slice.35
  143.6 3.0 dynamic_update_slice.35
  152.3 2.8 dynamic_update_slice.35
  160.8 2.8 dynamic_update_slice.35
  169.3 3.1 dynamic_update_slice.35
  178.1 3.1 dynamic_update_slice.35
  186.8 3.1 dynamic_update_slice.35
  195.6 3.0 dynamic_update_slice.35
  204.3 3.0 dynamic_update_slice.35
  213.0 3.1 dynamic_update_slice.35
  221.8 2.9 dynamic_update_slice.35
  230.4 3.1 dynamic_update_slice.35
  239.2 3.1 dynamic_update_slice.35
  242.3 3.6 collective-permute-start.3
  250.7 28.2 %collective-permute-done.4 = f32[3,256,128]{2,1,0:T(8,128)S(1)} collective-permute-done((f32[3,256,128]{2,1,0:T(8,128)S(1)}, f32[3,256,128]{2,1,0:T(8,128)S(1)}, u32[]{:S(2)}, u32[]{:S(2)}) %collective-permute-start.4) | collective-permute-done | bytes 393248 | tf_op jit(solution)/shard_map/ppermute | solution.py:13
  279.0 4.7 collective-permute-done.5
  285.8 2.9 collective-permute-start.7
  290.7 7.7 collective-permute-done.8
  299.7 49.1 %while.65 = (s32[]{:T(128)}, f32[2,384,384]{2,1,0:T(8,128)}, s32[16,3]{0,1:T(4,128)S(1)}, f32[16,2,128,128]{3,2,1,0:T(8,128)S(1)}, s32[]{:T(128)}) while((s32[]{:T(128)}, f32[2,384,384]{2,1,0:T(8,128)}, s32[16,3]{0,1:T(4,128)S(1)}, f32[16,2,128,128]{3,2,1,0:T(8,128)S(1)}, s32[]{:T(128)}) %tuple.237), condition=%wide.while_cond.7, body=%wide.while_body.7.sunk | while | flops 2 | bytes 262261 | solution.py:139
  354.3 13.6 %while.62 = (s32[]{:T(128)}, f32[16,2,128,128]{3,2,1,0:T(8,128)}, pred[16]{0:T(512)(128)(4,1)S(1)}, bf16[16,2,128,128]{2,3,1,0:T(8,128)(2,1)S(1)}, bf16[2,2,128,...) while((s32[]{:T(128)}, f32[16,2,128,128]{3,2,1,0:T(8,128)}, ...), condition=%wide.region_11.12_spmd, body=%wide.region_7.11_spmd.sunk | while | flops 269615104 | bytes 5898981 | solution.py:94
  373.3 279.8 %all-reduce.3.cloned.1.call-done = f32[2,128,128]{2,1,0:T(8,128)} async-done(((f32[2,128,128]{2,1,0:T(8,128)}), f32[2,128,128]{2,1,0:T(8,128)}) %all-reduce.3.cloned.1.call-update) | async-done | bytes 131088 | tf_op jit(solution)/shard_map/psum | solution.py:202
  653.2 126.3 %while.63 = (s32[]{:T(128)}, f32[2,384,384]{2,1,0:T(8,128)S(1)}, s32[16,2]{0,1:T(2,128)S(1)}, f32[16,2,128,128]{3,2,1,0:T(8,128)}, s32[]{:T(128)}, /*index=5*/s32[]{:T(128)}, s32[]{:T(128)}) while((s32[]{:T(128)}, f32[2,384,384]{2,1,0:T(8,128)S(1)}, s32[16,2]{0,1:T(2,128)S(1)}, f32[16,2,128,128]{3,2,1,0:T(8,128)}, s32[]{:T(128)}, ...), condition=%wide.region_13.14_spmd, body=%wide.region_12.13_spmd.sunk | while | flops 32776 | bytes 655557 | solution.py:162
  728.9 2.5 dynamic_update_slice.37
  780.3 17.4 %collective-permute-start.9 = (f32[2,128,256]{2,1,0:T(8,128)}, f32[2,128,256]{2,1,0:T(8,128)S(1)}, u32[]{:S(2)}, u32[]{:S(2)}) collective-permute-start(f32[2,128,256]{2,1,0:T(8,128)} %slice.375), channel_id=1, source_target_pairs={{0,32},{32,64},{64,96},{96,128},{128,160},{160,192},{192,224},{224... | collective-permute-start | bytes 786440 | tf_op jit(solution)/shard_map/ppermute | solution.py:13
  805.3 14.8 %collective-permute-done.10 = f32[2,256,128]{2,1,0:T(8,128)} collective-permute-done((f32[2,256,128]{2,1,0:T(8,128)S(1)}, f32[2,256,128]{2,1,0:T(8,128)}, u32[]{:S(2)}, u32[]{:S(2)}) %collective-permute-start.10) | collective-permute-done | bytes 262176 | tf_op jit(solution)/shard_map/ppermute | solution.py:13
  (356 shorter events, 267.7 us)
Async XLA Ops:
  7.2 24.4 %copy-start.8 = (bf16[1,1,16,128,128]{4,3,2,1,0:T(8,128)(2,1)S(1)}, bf16[1,1,16,128,128]{4,3,2,1,0:T(8,128)(2,1)}, u32[]{:S(2)}) copy-start(bf16[1,1,16,128,128]{4,3,2,1,0:T(8,128)(2,1)} %param.31) | copy-start | bytes 1572868
  7.2 645.9 %all-reduce.3.cloned.1.call-start = ((), (), s32[]{:S(2)}) async-start(), calls=%async_computation | async-start | bytes 262144 | tf_op jit(solution)/shard_map/psum | solution.py:202
  8.2 25.5 %collective-permute-start = (f32[2,256,128]{2,1,0:T(8,128)S(1)}, f32[2,256,128]{2,1,0:T(8,128)S(1)}, u32[]{:S(2)}, u32[]{:S(2)}) collective-permute-start(f32[2,256,128]{2,1,0:T(8,128)S(1)} %slice.345), channel_id=1, source_target_pairs={{1,0},{2,1},{3,2},{4,3},{5,4},{6,5},{7,6},{8,7},{9,8},{10,9},{11,1... | collective-permute-start | bytes 786440 | tf_op jit(solution)/shard_map/ppermute | solution.py:13
  20.6 13.2 %copy-start.4 = (f32[2,256,256]{2,1,0:T(8,128)S(1)}, f32[2,256,256]{2,1,0:T(8,128)}, u32[]{:S(2)}) copy-start(f32[2,256,256]{2,1,0:T(8,128)} %param.29) | copy-start | bytes 1572868
  20.6 13.2 %collective-permute-start.1 = (f32[2,128,256]{2,1,0:T(8,128)S(1)}, f32[2,128,256]{2,1,0:T(8,128)S(1)}, u32[]{:S(2)}, u32[]{:S(2)}) collective-permute-start(f32[2,128,256]{2,1,0:T(8,128)S(1)} %slice.346), channel_id=1, source_target_pairs={{32,0},{64,32},{96,64},{128,96},{160,128},{192,160},{224,192},{256... | collective-permute-start | bytes 786440 | tf_op jit(solution)/shard_map/ppermute | solution.py:13
  24.5 9.2 %collective-permute-start.2 = (f32[2,128,128]{2,1,0:T(8,128)S(1)}, f32[2,128,128]{2,1,0:T(8,128)S(1)}, u32[]{:S(2)}, u32[]{:S(2)}) collective-permute-start(f32[2,128,128]{2,1,0:T(8,128)S(1)} %slice.347), channel_id=1, source_target_pairs={{33,0},{34,1},{35,2},{36,3},{37,4},{38,5},{39,6},{40,7},{41,8},{42... | collective-permute-start | bytes 393224 | tf_op jit(solution)/shard_map/ppermute | solution.py:13
  99.5 2.1 copy-start.3
  101.6 1.2 copy-start.6
  102.8 2.0 copy-start.9
  242.3 8.3 %collective-permute-start.3 = (f32[3,128,256]{2,1,0:T(8,128)S(1)}, f32[3,128,256]{2,1,0:T(8,128)S(1)}, u32[]{:S(2)}, u32[]{:S(2)}) collective-permute-start(f32[3,128,256]{2,1,0:T(8,128)S(1)} %slice.359), channel_id=1, source_target_pairs={{0,32},{32,64},{64,96},{96,128},{128,160},{160,192},{192,224},{224... | collective-permute-start | bytes 1179656 | tf_op jit(solution)/shard_map/ppermute | solution.py:13
  245.9 32.9 %collective-permute-start.4 = (f32[3,256,128]{2,1,0:T(8,128)S(1)}, f32[3,256,128]{2,1,0:T(8,128)S(1)}, u32[]{:S(2)}, u32[]{:S(2)}) collective-permute-start(f32[3,256,128]{2,1,0:T(8,128)S(1)} %slice.361), channel_id=1, source_target_pairs={{0,1},{1,2},{2,3},{3,4},{4,5},{5,6},{6,7},{7,8},{8,9},{9,10},{10,1... | collective-permute-start | bytes 1179656 | tf_op jit(solution)/shard_map/ppermute | solution.py:13
  247.9 35.8 %copy-start.5 = (f32[2,256,256]{2,1,0:T(8,128)S(1)}, f32[2,256,256]{2,1,0:T(8,128)}, u32[]{:S(2)}) copy-start(f32[2,256,256]{2,1,0:T(8,128)} %param.29) | copy-start | bytes 1572868
  248.0 35.7 %collective-permute-start.5 = (f32[3,128,128]{2,1,0:T(8,128)S(1)}, f32[3,128,128]{2,1,0:T(8,128)S(1)}, u32[]{:S(2)}, u32[]{:S(2)}) collective-permute-start(f32[3,128,128]{2,1,0:T(8,128)S(1)} %slice.363), channel_id=1, source_target_pairs={{0,33},{1,34},{2,35},{3,36},{4,37},{5,38},{6,39},{7,40},{8,41},{9,... | collective-permute-start | bytes 589832 | tf_op jit(solution)/shard_map/ppermute | solution.py:13
  283.9 14.5 %collective-permute-start.6 = (f32[2,256,128]{2,1,0:T(8,128)S(1)}, f32[2,256,128]{2,1,0:T(8,128)S(1)}, u32[]{:S(2)}, u32[]{:S(2)}) collective-permute-start(f32[2,256,128]{2,1,0:T(8,128)S(1)} %slice.424), channel_id=1, source_target_pairs={{1,0},{2,1},{3,2},{4,3},{5,4},{6,5},{7,6},{8,7},{9,8},{10,9},{11,1... | collective-permute-start | bytes 786440 | tf_op jit(solution)/shard_map/ppermute | solution.py:13
  285.8 12.5 %collective-permute-start.7 = (f32[2,128,256]{2,1,0:T(8,128)S(1)}, f32[2,128,256]{2,1,0:T(8,128)S(1)}, u32[]{:S(2)}, u32[]{:S(2)}) collective-permute-start(f32[2,128,256]{2,1,0:T(8,128)S(1)} %slice.425), channel_id=1, source_target_pairs={{32,0},{64,32},{96,64},{128,96},{160,128},{192,160},{224,192},{256... | collective-permute-start | bytes 786440 | tf_op jit(solution)/shard_map/ppermute | solution.py:13
  288.7 9.6 %collective-permute-start.8 = (f32[2,128,128]{2,1,0:T(8,128)S(1)}, f32[2,128,128]{2,1,0:T(8,128)S(1)}, u32[]{:S(2)}, u32[]{:S(2)}) collective-permute-start(f32[2,128,128]{2,1,0:T(8,128)S(1)} %slice.426), channel_id=1, source_target_pairs={{33,0},{34,1},{35,2},{36,3},{37,4},{38,5},{39,6},{40,7},{41,8},{42... | collective-permute-start | bytes 393224 | tf_op jit(solution)/shard_map/ppermute | solution.py:13
  348.8 1.6 copy-start
  352.7 1.6 copy-start.2
  367.9 2.2 copy-start.1
  371.7 429.8 %all-reduce.5.cloned.1.call-start = ((), (), s32[]{:S(2)}) async-start(), calls=%async_computation.1 | async-start | bytes 262144 | tf_op jit(solution)/shard_map/psum | solution.py:203
  779.4 24.3 %copy-start.7 = (f32[2,128,128]{2,1,0:T(8,128)S(1)}, f32[2,128,128]{2,1,0:T(8,128)}, u32[]{:S(2)}) copy-start(f32[2,128,128]{2,1,0:T(8,128)} %param.30) | copy-start | bytes 393220
  780.3 25.0 %collective-permute-start.9 = (f32[2,128,256]{2,1,0:T(8,128)}, f32[2,128,256]{2,1,0:T(8,128)S(1)}, u32[]{:S(2)}, u32[]{:S(2)}) collective-permute-start(f32[2,128,256]{2,1,0:T(8,128)} %slice.375), channel_id=1, source_target_pairs={{0,32},{32,64},{64,96},{96,128},{128,160},{160,192},{192,224},{224... | collective-permute-start | bytes 786440 | tf_op jit(solution)/shard_map/ppermute | solution.py:13
  797.6 22.5 %collective-permute-start.10 = (f32[2,256,128]{2,1,0:T(8,128)S(1)}, f32[2,256,128]{2,1,0:T(8,128)}, u32[]{:S(2)}, u32[]{:S(2)}) collective-permute-start(f32[2,256,128]{2,1,0:T(8,128)S(1)} %slice.377), channel_id=1, source_target_pairs={{0,1},{1,2},{2,3},{3,4},{4,5},{5,6},{6,7},{7,8},{8,9},{9,10},{10,1... | collective-permute-start | bytes 786440 | tf_op jit(solution)/shard_map/ppermute | solution.py:13
  799.6 23.0 %collective-permute-start.11 = (f32[2,128,128]{2,1,0:T(8,128)S(1)}, f32[2,128,128]{2,1,0:T(8,128)S(1)}, u32[]{:S(2)}, u32[]{:S(2)}) collective-permute-start(f32[2,128,128]{2,1,0:T(8,128)S(1)} %slice.379), channel_id=1, source_target_pairs={{0,33},{1,34},{2,35},{3,36},{4,37},{5,38},{6,39},{7,40},{8,41},{9,... | collective-permute-start | bytes 393224 | tf_op jit(solution)/shard_map/ppermute | solution.py:13
Sparse Core Ops, SparseCore 0:
  371.9 281.1 all-reduce.2
  655.9 134.7 all-reduce.4
